TPU v7x, 32 devices: a whole 2x2x4 slice. The times are simulated.
32 devices in a mesh: orb: 16 (over z, y, core), grid: 2 (over x).
Axes of the slice: x: 2, y: 2, z: 4, core: 2. Of those that a mesh axis runs over, the one named last changes fastest.
Arguments:
- orbitals: bfloat16 [32, 11520], P('orb', 'grid'), may hold values from -1.5 to 1.5
- occupation: bfloat16 [32], P('orb'), may hold values from 0.29882812 to 1
Outputs:
- potentials: float32 [32, 11520], P('orb', 'grid')
- projectors: float32 [32, 11520], P('orb', 'grid')
All inputs are finite; a program needn't handle non-finite values.
Results may differ from a plain program's by a relative error of at most 0.0025.
Values may be sent and summed in bfloat16 or wider, within the bound.
No kernel may reach another device: no remote copies, remote signals or barrier semaphores. Data moves between devices by JAX's collectives and lax.ppermute only.
A program may use at most 64 MiB of HBM per device.

v0:
```python
import math
import jax
import jax.numpy as jnp
from jax import lax
from jax.sharding import PartitionSpec as P

NX = 20
NY = 24
NZ = 24
NPTS = 11520


def hartley_table(length):
    index = jnp.arange(length, dtype=jnp.int32)
    product = index[:, None] * index[None, :] % length
    angle = 2.0 * math.pi / length * product.astype(jnp.float32)
    return (jnp.cos(angle) + jnp.sin(angle)).astype(jnp.bfloat16)


def signed_square(length):
    index = jnp.arange(length, dtype=jnp.int32)
    signed = jnp.where(index <= length // 2, index, index - length).astype(jnp.float32)
    return (2.0 * math.pi * signed / length) ** 2


def coulomb_kernel(size_x, size_y, size_z):
    total = (
        signed_square(size_x)[:, None, None]
        + signed_square(size_y)[None, :, None]
        + signed_square(size_z)[None, None, :]
    )
    safe = jnp.where(total > 0, total, 1.0)
    return jnp.where(total > 0, 1.0 / safe, 0.0) / (size_x * size_y * size_z)


def solve_pairs(density, table_x, table_y, table_z, kernel):
    section = jnp.einsum(
        "ax,pxyz->payz", table_x, density, preferred_element_type=jnp.float32
    ).astype(jnp.bfloat16)
    section = jnp.einsum(
        "by,pxyz->pxbz", table_y, section, preferred_element_type=jnp.float32
    ).astype(jnp.bfloat16)
    spectrum = jnp.einsum("cz,pxyz->pxyc", table_z, section, preferred_element_type=jnp.float32)
    section = (spectrum * kernel).astype(jnp.bfloat16)
    section = jnp.einsum(
        "cz,pxyz->pxyc", table_z, section, preferred_element_type=jnp.float32
    ).astype(jnp.bfloat16)
    section = jnp.einsum(
        "by,pxyz->pxbz", table_y, section, preferred_element_type=jnp.float32
    ).astype(jnp.bfloat16)
    return jnp.einsum("ax,pxyz->payz", table_x, section, preferred_element_type=jnp.float32)


def pair_folder(targets, running, pieces):
    table_x = hartley_table(NX)
    table_y = hartley_table(NY)
    table_z = hartley_table(NZ)
    kernel = coulomb_kernel(NX, NY, NZ)
    target_rows = targets.astype(jnp.float32)
    target_count = targets.shape[0]
    block, block_weight = pieces
    rows = block.shape[0]
    group = math.gcd(rows, 64)
    blocks = block.reshape(rows // group, group, NPTS)
    weights = block_weight.astype(jnp.float32).reshape(rows // group, group)

    def accumulate(totals, inputs):
        sources, source_weight = inputs
        source_rows = sources.astype(jnp.float32)
        density = (target_rows[:, None, :] * source_rows[None, :, :]).astype(jnp.bfloat16)
        density = density.reshape(target_count * group, NX, NY, NZ)
        potential = solve_pairs(density, table_x, table_y, table_z, kernel).reshape(
            target_count, group, NPTS
        )
        weighted = source_weight[None, :, None] * potential * source_rows[None, :, :]
        return (totals - jnp.sum(weighted, axis=1), None)

    result, unused = lax.scan(accumulate, running, (blocks, weights))
    return result


def on_device(orbitals, occupation):
    own_count = orbitals.shape[0]
    per_device = own_count // lax.axis_size("grid")
    empty = jnp.zeros((per_device, NPTS), jnp.float32)
    whole = lax.all_gather(orbitals, "grid", axis=1, tiled=True)
    targets = lax.dynamic_slice_in_dim(whole, lax.axis_index("grid") * per_device, per_device, 0)
    totals = pair_folder(
        targets,
        empty,
        (
            lax.all_gather(whole, "orb", axis=0, tiled=True),
            lax.all_gather(occupation, "orb", axis=0, tiled=True),
        ),
    )
    potentials = lax.all_to_all(totals, "grid", split_axis=1, concat_axis=0, tiled=True)
    source_points, potential_points = (
        lax.all_to_all(
            orbitals.astype(jnp.float32), "orb", split_axis=1, concat_axis=0, tiled=True
        ),
        lax.all_to_all(potentials, "orb", split_axis=1, concat_axis=0, tiled=True),
    )
    partial_gram = (
        lax.dot_general(
            source_points,
            potential_points,
            (((1,), (1,)), ((), ())),
            precision=lax.Precision.HIGHEST,
        )
        / NPTS
    )
    gram = lax.psum(partial_gram, ("orb", "grid"))
    factor = jnp.linalg.cholesky(-gram)
    identity = jnp.eye(gram.shape[0], dtype=jnp.float32)
    inverse = lax.linalg.triangular_solve(factor, identity, left_side=True, lower=True)
    projector_points = jnp.dot(inverse, potential_points, precision=lax.Precision.HIGHEST)
    projectors = lax.all_to_all(projector_points, "orb", split_axis=0, concat_axis=1, tiled=True)
    return (potentials, projectors)


def solution(mesh):
    placed = (P("orb", "grid"), P("orb"))
    return jax.shard_map(
        on_device,
        mesh=mesh,
        in_specs=placed,
        out_specs=(P("orb", "grid"), P("orb", "grid")),
        check_vma=False,
    )
```

profile of v0, /device:TPU:0, one launch (start us, length us, event | category | flops | bytes accessed | tf_op | source)
XLA Modules:
  0.0 226.1 jit_solution(919936937522886090)
XLA Ops:
  0.7 5.7 %all_gather.10 = bf16[2,11520]{1,0:T(2,128)(2,1)S(1)} all-gather(bf16[2,5760]{1,0:T(2,128)(2,1)} %param.2), channel_id=1, replica_groups=mesh['orb'=16,'grid'=2] {'grid'}, dimensions={1}, use_global_device_ids=true | all-gather | bytes 69120 | tf_op jit(solution)/shard_map/all_gather | solution.py:86
  6.3 24.3 %all-gather = bf16[16,2,11520]{2,1,0:T(2,128)(2,1)S(1)} all-gather(bf16[1,2,11520]{2,1,0:T(2,128)(2,1)S(1)} %bitcast.58), channel_id=1, replica_groups=mesh['orb'=16,'grid'=2] {'orb'}, dimensions={0}, use_global_device_ids=true | all-gather | bytes 783360 | tf_op jit(solution)/shard_map/all_gather | solution.py:92
  30.7 6.4 %reshape.167 = f32[32,20,24,24]{3,2,1,0:T(8,128)} reshape(bf16[16,2,11520]{2,1,0:T(2,128)(2,1)S(1)} %all-gather) | data formatting | bytes 2211840 | tf_op jit(solution)/shard_map/while/body/eval_jaxpr/convert_element_type | solution.py:69
  37.1 1.3 reshape.174
  38.4 0.1 convert_reduce_fusion
  38.6 0.2 reshape.166
  38.8 3.9 %multiply_convert_fusion.1 = bf16[32,20,24,24]{3,2,1,0:T(8,128)(2,1)S(1)} fusion(f32[32,20,24,24]{3,2,1,0:T(8,128)} %reshape.167, f32[20,24,24]{2,1,0:T(8,128)S(1)} %reshape.166), kind=kLoop, calls=%fused_computation.1 | loop fusion | flops 737280 | bytes 2257920 | tf_op jit(solution)/shard_map/while/body/eval_jaxpr/convert_element_type | solution.py:70
  42.6 4.9 %convert_bitcast_fusion = bf16[32,20,24,24]{1,3,2,0:T(8,128)(2,1)} fusion(bf16[32,20,24,24]{3,2,1,0:T(8,128)(2,1)S(1)} %multiply_convert_fusion.1), kind=kOutput, calls=%fused_computation.4 | convolution fusion | flops 15118640 | bytes 1474560 | tf_op jit(solution)/shard_map/while/body/eval_jaxpr/ax,pxyz->payz/dot_general | solution.py:37
  47.5 8.5 %copy.24 = bf16[32,20,24,24]{2,3,1,0:T(8,128)(2,1)} copy(bf16[32,20,24,24]{1,3,2,0:T(8,128)(2,1)} %convert_bitcast_fusion) | data formatting | bytes 1474560 | tf_op jit(solution)/shard_map/while/body/eval_jaxpr/convert_element_type | solution.py:39
  56.0 5.2 %fusion.44 = bf16[32,20,24,24]{3,2,1,0:T(8,128)(2,1)} fusion(bf16[32,20,24,24]{2,3,1,0:T(8,128)(2,1)} %copy.24), kind=kOutput, calls=%fused_computation.53 | convolution fusion | flops 17701056 | bytes 1474560 | tf_op jit(solution)/shard_map/while/body/eval_jaxpr/by,pxyz->pxbz/dot_general | solution.py:40
  61.3 0.1 fusion.19
  61.5 7.4 %fusion.2 = bf16[32,20,24,24]{3,2,1,0:T(8,128)(2,1)} fusion(f32[20,24,24]{2,1,0:T(8,128)S(1)} %fusion.19, bf16[32,20,24,24]{3,2,1,0:T(8,128)(2,1)} %fusion.44), kind=kOutput, calls=%fused_computation.5 | convolution fusion | flops 36139392 | bytes 1520640 | tf_op jit(solution)/shard_map/while/body/eval_jaxpr/cz,pxyz->pxyc/dot_general | solution.py:45
  68.9 5.4 %convert_bitcast_fusion.1 = bf16[32,20,24,24]{2,3,1,0:T(8,128)(2,1)} fusion(bf16[32,20,24,24]{3,2,1,0:T(8,128)(2,1)} %fusion.2), kind=kOutput, calls=%fused_computation.8 | convolution fusion | flops 18069696 | bytes 1474560 | tf_op jit(solution)/shard_map/while/body/eval_jaxpr/by,pxyz->pxbz/dot_general | solution.py:48
  74.3 10.1 %copy.27 = bf16[32,20,24,24]{0,1,3,2:T(8,128)(2,1)S(1)} copy(bf16[32,20,24,24]{2,3,1,0:T(8,128)(2,1)} %convert_bitcast_fusion.1) | data formatting | bytes 1474560 | tf_op jit(solution)/shard_map/while/body/eval_jaxpr/convert_element_type | solution.py:50
  84.4 4.0 %convolution_bitcast_fusion = f32[32,20,24,24]{0,1,3,2:T(8,128)} fusion(bf16[32,20,24,24]{0,1,3,2:T(8,128)(2,1)S(1)} %copy.27), kind=kOutput, calls=%fused_computation.13 | convolution fusion | flops 14750000 | bytes 2211840 | tf_op jit(solution)/shard_map/while/body/eval_jaxpr/ax,pxyz->payz/dot_general | solution.py:51
  88.4 12.1 %copy.28 = f32[32,20,24,24]{3,2,1,0:T(8,128)} copy(f32[32,20,24,24]{0,1,3,2:T(8,128)} %convolution_bitcast_fusion) | data formatting | bytes 2949120 | tf_op jit(solution)/shard_map/while/body/eval_jaxpr/ax,pxyz->payz/transpose | solution.py:51
  100.5 0.6 dynamic-slice
  101.8 0.2 dynamic-update-slice.3
  102.0 6.8 %reshape.165 = f32[32,11520]{1,0:T(8,128)S(1)} reshape(f32[32,20,24,24]{3,2,1,0:T(8,128)} %copy.28) | data formatting | bytes 2949120 | tf_op jit(solution)/shard_map/while/body/eval_jaxpr/reshape | solution.py:72
  108.9 29.9 %all-reduce = bf16[32]{0:T(256)(128)(2,1)S(1)} all-reduce(bf16[32]{0:T(256)(128)(2,1)S(1)} %dynamic-update-slice.3), channel_id=1, replica_groups=mesh['orb'=16,'grid'=2] {'orb'}, use_global_device_ids=true, to_apply=%add | all-reduce | flops 32 | bytes 128
  138.8 0.3 multiply_reduce_fusion
  139.1 0.7 sub.25
  139.7 3.3 %all-to-all-start = ((f32[1,2,5760]{2,0,1:T(1,128)}), f32[1,2,5760]{2,0,1:T(1,128)S(1)}, u32[]{:S(2)}, u32[]{:S(2)}) async-start(f32[1,2,5760]{2,0,1:T(1,128)} %sub.25), calls=%async_computation | async-start | bytes 92160 | tf_op jit(solution)/shard_map/all_to_all | solution.py:96
  143.0 0.1 reshape.168
  143.2 0.6 copy.30
  143.8 3.2 %all-to-all-done = f32[1,2,5760]{2,0,1:T(1,128)S(1)} async-done(((f32[1,2,5760]{2,0,1:T(1,128)}), f32[1,2,5760]{2,0,1:T(1,128)S(1)}, u32[]{:S(2)}, u32[]{:S(2)}) %all-to-all-start) | async-done | bytes 46112 | tf_op jit(solution)/shard_map/all_to_all | solution.py:96
  147.0 3.5 %all-to-all-start.2 = ((f32[2,16,360]{2,0,1:T(2,128)}), f32[2,16,360]{2,0,1:T(2,128)S(1)}, u32[]{:S(2)}, u32[]{:S(2)}) async-start(f32[2,16,360]{2,0,1:T(2,128)} %copy.30), calls=%async_computation.2 | async-start | bytes 98304 | tf_op jit(solution)/shard_map/all_to_all | solution.py:98
  150.5 0.1 reduce.11
  150.7 0.1 all_to_all.54
  150.8 0.6 copy.29
  151.4 5.8 %all-to-all-done.2 = f32[2,16,360]{2,0,1:T(2,128)S(1)} async-done(((f32[2,16,360]{2,0,1:T(2,128)}), f32[2,16,360]{2,0,1:T(2,128)S(1)}, u32[]{:S(2)}, u32[]{:S(2)}) %all-to-all-start.2) | async-done | bytes 46112 | tf_op jit(solution)/shard_map/all_to_all | solution.py:98
  157.3 3.5 %all-to-all-start.1 = ((f32[2,16,360]{2,0,1:T(2,128)}), f32[2,16,360]{2,0,1:T(2,128)S(1)}, u32[]{:S(2)}, u32[]{:S(2)}) async-start(f32[2,16,360]{2,0,1:T(2,128)} %copy.29), calls=%async_computation.1 | async-start | bytes 98304 | tf_op jit(solution)/shard_map/all_to_all | solution.py:101
  160.8 6.7 %all-to-all-done.1 = f32[2,16,360]{2,0,1:T(2,128)S(1)} async-done(((f32[2,16,360]{2,0,1:T(2,128)}), f32[2,16,360]{2,0,1:T(2,128)S(1)}, u32[]{:S(2)}, u32[]{:S(2)}) %all-to-all-start.1) | async-done | bytes 46112 | tf_op jit(solution)/shard_map/all_to_all | solution.py:101
  167.6 0.2 fusion.17
  167.8 38.0 %psum.7 = f32[32,32]{0,1:T(8,128)S(1)} all-reduce(f32[32,32]{0,1:T(8,128)S(1)} %fusion.17), channel_id=1, replica_groups=mesh['orb'=16,'grid'=2] {'orb','grid'}, use_global_device_ids=true, to_apply=%region_1.2 | all-reduce | flops 1024 | bytes 8192 | tf_op jit(solution)/shard_map/psum | solution.py:112
  205.8 0.1 copy.31
  205.8 2.9 %cholesky.17 = f32[32,32]{1,0:T(8,128)S(1)} custom-call(f32[32,32]{1,0:T(8,128)S(1)} %fusion.22), custom_call_target="Cholesky" | custom-call | tf_op jit(solution)/shard_map/jit(cholesky)/cholesky | solution.py:113
  208.8 0.6 compare_reduce_fusion
  209.4 0.7 fusion.21
  210.1 2.4 %custom-call.6 = f32[1,32,32]{1,2,0:T(8,128)S(1)} custom-call(f32[1,32,32]{2,1,0:T(8,128)S(1)} %fusion.21), custom_call_target="InvertDiagBlocksLowerTriangular" | custom-call | tf_op jit(solution)/shard_map/triangular_solve | solution.py:115
  212.5 0.1 copy.32
  212.6 0.2 fusion.23
  212.8 0.2 fusion.88
  213.0 0.6 copy.34
  213.6 5.0 %all-to-all-start.3 = ((f32[16,2,360]{2,1,0:T(2,128)}), f32[16,2,360]{2,1,0:T(2,128)S(1)}, u32[]{:S(2)}, u32[]{:S(2)}) async-start(f32[16,2,360]{2,1,0:T(2,128)} %copy.34), calls=%async_computation.3 | async-start | bytes 98304 | tf_op jit(solution)/shard_map/all_to_all | solution.py:117
  218.6 0.6 copy.48
  219.3 6.1 %all-to-all-done.3 = f32[16,2,360]{2,1,0:T(2,128)S(1)} async-done(((f32[16,2,360]{2,1,0:T(2,128)}), f32[16,2,360]{2,1,0:T(2,128)S(1)}, u32[]{:S(2)}, u32[]{:S(2)}) %all-to-all-start.3) | async-done | bytes 46112 | tf_op jit(solution)/shard_map/all_to_all | solution.py:117
  225.4 0.8 all_to_all.65
  (21 shorter events, 0.3 us)
Async XLA Ops:
  88.4 12.1 %copy-start.3 = (u32[32]{0:T(128)S(1)}, u32[32]{0:T(128)}, u32[]{:S(2)}) copy-start(u32[32]{0:T(128)} %constant.125) | copy-start | bytes 388
  88.4 13.4 %copy-start.2 = (bf16[2]{0:T(256)(128)(2,1)S(1)}, bf16[2]{0:T(256)(128)(2,1)}, u32[]{:S(2)}) copy-start(bf16[2]{0:T(256)(128)(2,1)} %param.3) | copy-start | bytes 16
  102.0 36.7 %copy-start = (f32[32,11520]{1,0:T(8,128)S(1)}, f32[32,11520]{1,0:T(8,128)}, u32[]{:S(2)}) copy-start(f32[32,11520]{1,0:T(8,128)} %reshape.174) | copy-start | bytes 4423684
  102.0 41.0 %copy-start.1 = (bf16[2,5760]{1,0:T(2,128)(2,1)S(1)}, bf16[2,5760]{1,0:T(2,128)(2,1)}, u32[]{:S(2)}) copy-start(bf16[2,5760]{1,0:T(2,128)(2,1)} %param.2) | copy-start | bytes 69124
  139.7 7.3 %all-to-all-start = ((f32[1,2,5760]{2,0,1:T(1,128)}), f32[1,2,5760]{2,0,1:T(1,128)S(1)}, u32[]{:S(2)}, u32[]{:S(2)}) async-start(f32[1,2,5760]{2,0,1:T(1,128)} %sub.25), calls=%async_computation | async-start | bytes 92160 | tf_op jit(solution)/shard_map/all_to_all | solution.py:96
  147.0 10.2 %all-to-all-start.2 = ((f32[2,16,360]{2,0,1:T(2,128)}), f32[2,16,360]{2,0,1:T(2,128)S(1)}, u32[]{:S(2)}, u32[]{:S(2)}) async-start(f32[2,16,360]{2,0,1:T(2,128)} %copy.30), calls=%async_computation.2 | async-start | bytes 98304 | tf_op jit(solution)/shard_map/all_to_all | solution.py:98
  157.3 10.2 %all-to-all-start.1 = ((f32[2,16,360]{2,0,1:T(2,128)}), f32[2,16,360]{2,0,1:T(2,128)S(1)}, u32[]{:S(2)}, u32[]{:S(2)}) async-start(f32[2,16,360]{2,0,1:T(2,128)} %copy.29), calls=%async_computation.1 | async-start | bytes 98304 | tf_op jit(solution)/shard_map/all_to_all | solution.py:101
  213.6 11.8 %all-to-all-start.3 = ((f32[16,2,360]{2,1,0:T(2,128)}), f32[16,2,360]{2,1,0:T(2,128)S(1)}, u32[]{:S(2)}, u32[]{:S(2)}) async-start(f32[16,2,360]{2,1,0:T(2,128)} %copy.34), calls=%async_computation.3 | async-start | bytes 98304 | tf_op jit(solution)/shard_map/all_to_all | solution.py:117
where the time goes:
time: 227 us; the launch traced here: 226 us
  blocking collectives  97.9 us (43%)
  local copies, waits for them, and re-layouts  50.8 us (22%)
  matrix products  27.5 us (12%)
  waiting for transfers between devices  21.9 us (10%)
  starting transfers between devices  15.3 us (7%)
  other arithmetic  11.4 us (5%)
    psum x1, blocking collectives, on_device(): gram = lax.psum(partial_gram, ('orb', 'grid'))  38 us
    unnamed x1, blocking collectives  29.9 us
    all_gather x1, blocking collectives, on_device(): lax.all_gather(whole, 'orb', axis=0, tiled=True)  24.3 us
    transpose x1, local copies, waits for them, and re-layouts, solve_pairs(): jnp.einsum('ax,pxyz->payz', table_x, section, preferred_element_type=jnp....  12.1 us
    dot_general x2, matrix products, solve_pairs(): jnp.einsum('by,pxyz->pxbz', table_y, section, preferred_element_type=jnp....  10.6 us
    convert_element_type x1, local copies, waits for them, and re-layouts, solve_pairs(): section = jnp.einsum('by,pxyz->pxbz', table_y, section, preferred_element...  10.1 us
    convert_element_type x1, local copies, waits for them, and re-layouts, solve_pairs(): section = jnp.einsum('ax,pxyz->payz', table_x, density, preferred_element...  8.51 us
    convert_element_type x2, local copies, waits for them, and re-layouts, accumulate(): source_rows = sources.astype(jnp.float32)  7.76 us
  transfers between devices with their start and end apart: 4, of which 4 were waited for; matrix products, arithmetic and copies ran while one was open for 1% of the time, Pallas kernels for 0%

commit v1 on v0

--- a/solution.py
+++ b/solution.py
@@ -109,7 +109,7 @@
         )
         / NPTS
     )
-    gram = lax.psum(partial_gram, ("orb", "grid"))
+    gram = jnp.sum(lax.all_gather(partial_gram, ("orb", "grid")), axis=0)
     factor = jnp.linalg.cholesky(-gram)
     identity = jnp.eye(gram.shape[0], dtype=jnp.float32)
     inverse = lax.linalg.triangular_solve(factor, identity, left_side=True, lower=True)

time: 227 us -> 254 us (1.12)
  blocking collectives: 97.9 us -> 126 us
    all_gather x0 -> x1, blocking collectives: none -> 66.3 us  [on_device(): gram = jnp.sum(lax.all_gather(partial_gram, ('orb', 'grid')), axis=0)]
    psum x1 -> x0, blocking collectives: 38 us -> none  [on_device(): gram = lax.psum(partial_gram, ('orb', 'grid'))]
where the time goes in v1:
time: 254 us; the launch traced here: 253 us
  blocking collectives  126 us (50%)
  local copies, waits for them, and re-layouts  51 us (20%)
  matrix products  27.5 us (11%)
  waiting for transfers between devices  21.8 us (9%)
  starting transfers between devices  13.8 us (5%)
  other arithmetic  11.4 us (4%)
    all_gather x1, blocking collectives, on_device(): gram = jnp.sum(lax.all_gather(partial_gram, ('orb', 'grid')), axis=0)  66.3 us
    unnamed x1, blocking collectives  29.9 us
    all_gather x1, blocking collectives, on_device(): lax.all_gather(whole, 'orb', axis=0, tiled=True)  24.3 us
    transpose x1, local copies, waits for them, and re-layouts, solve_pairs(): jnp.einsum('ax,pxyz->payz', table_x, section, preferred_element_type=jnp....  12.1 us
    dot_general x2, matrix products, solve_pairs(): jnp.einsum('by,pxyz->pxbz', table_y, section, preferred_element_type=jnp....  10.6 us
    convert_element_type x1, local copies, waits for them, and re-layouts, solve_pairs(): section = jnp.einsum('by,pxyz->pxbz', table_y, section, preferred_element...  10.1 us
    convert_element_type x1, local copies, waits for them, and re-layouts, solve_pairs(): section = jnp.einsum('ax,pxyz->payz', table_x, density, preferred_element...  8.51 us
    convert_element_type x2, local copies, waits for them, and re-layouts, accumulate(): source_rows = sources.astype(jnp.float32)  7.76 us
  transfers between devices with their start and end apart: 4, of which 4 were waited for; matrix products, arithmetic and copies ran while one was open for 1% of the time, Pallas kernels for 0%

profile of v1, /device:TPU:0, one launch (start us, length us, event | category | flops | bytes accessed | tf_op | source)
XLA Modules:
  0.0 253.1 jit_solution(5391506182061745175)
XLA Ops:
  0.7 5.7 %all_gather.16 = bf16[2,11520]{1,0:T(2,128)(2,1)S(1)} all-gather(bf16[2,5760]{1,0:T(2,128)(2,1)} %param.2), channel_id=1, replica_groups=mesh['orb'=16,'grid'=2] {'grid'}, dimensions={1}, use_global_device_ids=true | all-gather | bytes 69120 | tf_op jit(solution)/shard_map/all_gather | solution.py:86
  6.3 24.3 %all-gather.1 = bf16[16,2,11520]{2,1,0:T(2,128)(2,1)S(1)} all-gather(bf16[1,2,11520]{2,1,0:T(2,128)(2,1)S(1)} %bitcast.60), channel_id=1, replica_groups=mesh['orb'=16,'grid'=2] {'orb'}, dimensions={0}, use_global_device_ids=true | all-gather | bytes 783360 | tf_op jit(solution)/shard_map/all_gather | solution.py:92
  30.7 6.4 %reshape.167 = f32[32,20,24,24]{3,2,1,0:T(8,128)} reshape(bf16[16,2,11520]{2,1,0:T(2,128)(2,1)S(1)} %all-gather.1) | data formatting | bytes 2211840 | tf_op jit(solution)/shard_map/while/body/eval_jaxpr/convert_element_type | solution.py:69
  37.1 1.3 reshape.175
  38.4 0.1 convert_reduce_fusion
  38.6 0.2 reshape.166
  38.8 3.9 %multiply_convert_fusion.1 = bf16[32,20,24,24]{3,2,1,0:T(8,128)(2,1)S(1)} fusion(f32[32,20,24,24]{3,2,1,0:T(8,128)} %reshape.167, f32[20,24,24]{2,1,0:T(8,128)S(1)} %reshape.166), kind=kLoop, calls=%fused_computation.1 | loop fusion | flops 737280 | bytes 2257920 | tf_op jit(solution)/shard_map/while/body/eval_jaxpr/convert_element_type | solution.py:70
  42.6 4.9 %convert_bitcast_fusion = bf16[32,20,24,24]{1,3,2,0:T(8,128)(2,1)} fusion(bf16[32,20,24,24]{3,2,1,0:T(8,128)(2,1)S(1)} %multiply_convert_fusion.1), kind=kOutput, calls=%fused_computation.4 | convolution fusion | flops 15118640 | bytes 1474560 | tf_op jit(solution)/shard_map/while/body/eval_jaxpr/ax,pxyz->payz/dot_general | solution.py:37
  47.5 8.5 %copy.39 = bf16[32,20,24,24]{2,3,1,0:T(8,128)(2,1)} copy(bf16[32,20,24,24]{1,3,2,0:T(8,128)(2,1)} %convert_bitcast_fusion) | data formatting | bytes 1474560 | tf_op jit(solution)/shard_map/while/body/eval_jaxpr/convert_element_type | solution.py:39
  56.0 5.2 %fusion.44 = bf16[32,20,24,24]{3,2,1,0:T(8,128)(2,1)} fusion(bf16[32,20,24,24]{2,3,1,0:T(8,128)(2,1)} %copy.39), kind=kOutput, calls=%fused_computation.53 | convolution fusion | flops 17701056 | bytes 1474560 | tf_op jit(solution)/shard_map/while/body/eval_jaxpr/by,pxyz->pxbz/dot_general | solution.py:40
  61.3 0.1 fusion.19
  61.5 7.4 %fusion.2 = bf16[32,20,24,24]{3,2,1,0:T(8,128)(2,1)} fusion(f32[20,24,24]{2,1,0:T(8,128)S(1)} %fusion.19, bf16[32,20,24,24]{3,2,1,0:T(8,128)(2,1)} %fusion.44), kind=kOutput, calls=%fused_computation.5 | convolution fusion | flops 36139392 | bytes 1520640 | tf_op jit(solution)/shard_map/while/body/eval_jaxpr/cz,pxyz->pxyc/dot_general | solution.py:45
  68.9 5.4 %convert_bitcast_fusion.1 = bf16[32,20,24,24]{2,3,1,0:T(8,128)(2,1)} fusion(bf16[32,20,24,24]{3,2,1,0:T(8,128)(2,1)} %fusion.2), kind=kOutput, calls=%fused_computation.8 | convolution fusion | flops 18069696 | bytes 1474560 | tf_op jit(solution)/shard_map/while/body/eval_jaxpr/by,pxyz->pxbz/dot_general | solution.py:48
  74.3 10.1 %copy.42 = bf16[32,20,24,24]{0,1,3,2:T(8,128)(2,1)S(1)} copy(bf16[32,20,24,24]{2,3,1,0:T(8,128)(2,1)} %convert_bitcast_fusion.1) | data formatting | bytes 1474560 | tf_op jit(solution)/shard_map/while/body/eval_jaxpr/convert_element_type | solution.py:50
  84.4 4.0 %convolution_bitcast_fusion = f32[32,20,24,24]{0,1,3,2:T(8,128)} fusion(bf16[32,20,24,24]{0,1,3,2:T(8,128)(2,1)S(1)} %copy.42), kind=kOutput, calls=%fused_computation.13 | convolution fusion | flops 14750000 | bytes 2211840 | tf_op jit(solution)/shard_map/while/body/eval_jaxpr/ax,pxyz->payz/dot_general | solution.py:51
  88.4 12.1 %copy.43 = f32[32,20,24,24]{3,2,1,0:T(8,128)} copy(f32[32,20,24,24]{0,1,3,2:T(8,128)} %convolution_bitcast_fusion) | data formatting | bytes 2949120 | tf_op jit(solution)/shard_map/while/body/eval_jaxpr/ax,pxyz->payz/transpose | solution.py:51
  100.5 0.6 dynamic-slice
  101.8 0.2 dynamic-update-slice.3
  102.0 6.8 %reshape.165 = f32[32,11520]{1,0:T(8,128)S(1)} reshape(f32[32,20,24,24]{3,2,1,0:T(8,128)} %copy.43) | data formatting | bytes 2949120 | tf_op jit(solution)/shard_map/while/body/eval_jaxpr/reshape | solution.py:72
  108.9 29.9 %all-reduce = bf16[32]{0:T(256)(128)(2,1)S(1)} all-reduce(bf16[32]{0:T(256)(128)(2,1)S(1)} %dynamic-update-slice.3), channel_id=1, replica_groups=mesh['orb'=16,'grid'=2] {'orb'}, use_global_device_ids=true, to_apply=%add | all-reduce | flops 32 | bytes 128
  138.8 0.3 multiply_reduce_fusion
  139.1 0.7 sub.25
  139.7 3.3 %all-to-all-start = ((f32[1,2,5760]{2,0,1:T(1,128)}), f32[1,2,5760]{2,0,1:T(1,128)S(1)}, u32[]{:S(2)}, u32[]{:S(2)}) async-start(f32[1,2,5760]{2,0,1:T(1,128)} %sub.25), calls=%async_computation | async-start | bytes 92160 | tf_op jit(solution)/shard_map/all_to_all | solution.py:96
  143.0 0.1 reshape.168
  143.2 0.6 copy.45
  143.8 3.2 %all-to-all-done = f32[1,2,5760]{2,0,1:T(1,128)S(1)} async-done(((f32[1,2,5760]{2,0,1:T(1,128)}), f32[1,2,5760]{2,0,1:T(1,128)S(1)}, u32[]{:S(2)}, u32[]{:S(2)}) %all-to-all-start) | async-done | bytes 46112 | tf_op jit(solution)/shard_map/all_to_all | solution.py:96
  147.0 3.5 %all-to-all-start.2 = ((f32[2,16,360]{2,0,1:T(2,128)}), f32[2,16,360]{2,0,1:T(2,128)S(1)}, u32[]{:S(2)}, u32[]{:S(2)}) async-start(f32[2,16,360]{2,0,1:T(2,128)} %copy.45), calls=%async_computation.2 | async-start | bytes 98304 | tf_op jit(solution)/shard_map/all_to_all | solution.py:98
  150.5 0.1 reduce.11
  150.7 0.1 all_to_all.54
  150.8 0.6 copy.44
  151.4 5.8 %all-to-all-done.2 = f32[2,16,360]{2,0,1:T(2,128)S(1)} async-done(((f32[2,16,360]{2,0,1:T(2,128)}), f32[2,16,360]{2,0,1:T(2,128)S(1)}, u32[]{:S(2)}, u32[]{:S(2)}) %all-to-all-start.2) | async-done | bytes 46112 | tf_op jit(solution)/shard_map/all_to_all | solution.py:98
  157.3 3.5 %all-to-all-start.1 = ((f32[2,16,360]{2,0,1:T(2,128)}), f32[2,16,360]{2,0,1:T(2,128)S(1)}, u32[]{:S(2)}, u32[]{:S(2)}) async-start(f32[2,16,360]{2,0,1:T(2,128)} %copy.44), calls=%async_computation.1 | async-start | bytes 98304 | tf_op jit(solution)/shard_map/all_to_all | solution.py:101
  160.8 6.7 %all-to-all-done.1 = f32[2,16,360]{2,0,1:T(2,128)S(1)} async-done(((f32[2,16,360]{2,0,1:T(2,128)}), f32[2,16,360]{2,0,1:T(2,128)S(1)}, u32[]{:S(2)}, u32[]{:S(2)}) %all-to-all-start.1) | async-done | bytes 46112 | tf_op jit(solution)/shard_map/all_to_all | solution.py:101
  167.6 0.2 fusion.17
  167.8 66.3 %all-gather = f32[1024,32]{1,0:T(8,128)S(1)} all-gather(f32[32,32]{1,0:T(8,128)S(1)} %copy.46), channel_id=2, replica_groups=mesh['orb'=16,'grid'=2] {'orb','grid'}, dimensions={0}, use_global_device_ids=true | all-gather | bytes 135168 | tf_op jit(solution)/shard_map/all_gather | solution.py:112
  234.3 0.1 copy.48
  234.4 2.9 %cholesky.17 = f32[32,32]{1,0:T(8,128)S(1)} custom-call(f32[32,32]{1,0:T(8,128)S(1)} %fusion.22), custom_call_target="Cholesky" | custom-call | tf_op jit(solution)/shard_map/jit(cholesky)/cholesky | solution.py:113
  237.3 0.6 compare_reduce_fusion
  238.0 0.7 fusion.21
  238.6 2.4 custom-call.6
  241.1 0.1 copy.49
  241.1 0.2 fusion.23
  241.3 0.2 fusion.88
  241.5 0.6 copy.51
  242.1 3.5 %all-to-all-start.3 = ((f32[16,2,360]{2,1,0:T(2,128)}), f32[16,2,360]{2,1,0:T(2,128)S(1)}, u32[]{:S(2)}, u32[]{:S(2)}) async-start(f32[16,2,360]{2,1,0:T(2,128)} %copy.51), calls=%async_computation.3 | async-start | bytes 98304 | tf_op jit(solution)/shard_map/all_to_all | solution.py:117
  245.6 0.6 copy.65
  246.3 6.1 %all-to-all-done.3 = f32[16,2,360]{2,1,0:T(2,128)S(1)} async-done(((f32[16,2,360]{2,1,0:T(2,128)}), f32[16,2,360]{2,1,0:T(2,128)S(1)}, u32[]{:S(2)}, u32[]{:S(2)}) %all-to-all-start.3) | async-done | bytes 46112 | tf_op jit(solution)/shard_map/all_to_all | solution.py:117
  252.4 0.8 all_to_all.65
  (24 shorter events, 0.5 us)
Async XLA Ops:
  88.4 12.1 %copy-start.3 = (u32[32]{0:T(128)S(1)}, u32[32]{0:T(128)}, u32[]{:S(2)}) copy-start(u32[32]{0:T(128)} %constant.125) | copy-start | bytes 388
  88.4 13.4 %copy-start.2 = (bf16[2]{0:T(256)(128)(2,1)S(1)}, bf16[2]{0:T(256)(128)(2,1)}, u32[]{:S(2)}) copy-start(bf16[2]{0:T(256)(128)(2,1)} %param.3) | copy-start | bytes 16
  102.0 36.7 %copy-start = (f32[32,11520]{1,0:T(8,128)S(1)}, f32[32,11520]{1,0:T(8,128)}, u32[]{:S(2)}) copy-start(f32[32,11520]{1,0:T(8,128)} %reshape.175) | copy-start | bytes 4423684
  102.0 41.0 %copy-start.1 = (bf16[2,5760]{1,0:T(2,128)(2,1)S(1)}, bf16[2,5760]{1,0:T(2,128)(2,1)}, u32[]{:S(2)}) copy-start(bf16[2,5760]{1,0:T(2,128)(2,1)} %param.2) | copy-start | bytes 69124
  139.7 7.3 %all-to-all-start = ((f32[1,2,5760]{2,0,1:T(1,128)}), f32[1,2,5760]{2,0,1:T(1,128)S(1)}, u32[]{:S(2)}, u32[]{:S(2)}) async-start(f32[1,2,5760]{2,0,1:T(1,128)} %sub.25), calls=%async_computation | async-start | bytes 92160 | tf_op jit(solution)/shard_map/all_to_all | solution.py:96
  147.0 10.2 %all-to-all-start.2 = ((f32[2,16,360]{2,0,1:T(2,128)}), f32[2,16,360]{2,0,1:T(2,128)S(1)}, u32[]{:S(2)}, u32[]{:S(2)}) async-start(f32[2,16,360]{2,0,1:T(2,128)} %copy.45), calls=%async_computation.2 | async-start | bytes 98304 | tf_op jit(solution)/shard_map/all_to_all | solution.py:98
  157.3 10.2 %all-to-all-start.1 = ((f32[2,16,360]{2,0,1:T(2,128)}), f32[2,16,360]{2,0,1:T(2,128)S(1)}, u32[]{:S(2)}, u32[]{:S(2)}) async-start(f32[2,16,360]{2,0,1:T(2,128)} %copy.44), calls=%async_computation.1 | async-start | bytes 98304 | tf_op jit(solution)/shard_map/all_to_all | solution.py:101
  242.1 10.2 %all-to-all-start.3 = ((f32[16,2,360]{2,1,0:T(2,128)}), f32[16,2,360]{2,1,0:T(2,128)S(1)}, u32[]{:S(2)}, u32[]{:S(2)}) async-start(f32[16,2,360]{2,1,0:T(2,128)} %copy.51), calls=%async_computation.3 | async-start | bytes 98304 | tf_op jit(solution)/shard_map/all_to_all | solution.py:117
